TPU v7x, 256 devices: a whole 4x4x8 slice. The times are simulated.
256 devices in a mesh: row: 16 (over x_lo, y, core), col: 16 (over x_hi, z).
Axes of the slice: x: 4 (x_hi: 2, x_lo: 2; x = x_hi * 2 + x_lo), y: 4, z: 8, core: 2. Of those that a mesh axis runs over, the one named last changes fastest.
Arguments:
- queries: bfloat16 [262144, 768], P(('row', 'col'))
- documents: bfloat16 [8192, 768], P(('row', 'col'))
- counts: int32 [256], P(('row', 'col')), may hold values from 2 to 32, as said below
- positives: int32 [262144], P(('row', 'col')), may hold values from 0 to 8191, as said below
Outputs:
- losses: float32 [262144], P(('row', 'col'))
Inputs may be any that keep to these rules, and one draw needn't show every extreme that they name: `counts`: some block has exactly 32 valid slots in every draw. Each names a valid slot: positives[i] % 32 < counts[positives[i] // 32].
All inputs are finite; a program needn't handle non-finite values.
Results may differ from a plain program's by a relative error of at most 0.0003.
Values may be sent and summed in bfloat16 or wider, within the bound.
No kernel may reach another device: no remote copies, remote signals or barrier semaphores. Data moves between devices by JAX's collectives and lax.ppermute only.
A program may use at most 128 MiB of HBM per device.

v0:
```python
import math

import jax
import jax.numpy as jnp
from jax import lax
from jax.sharding import Mesh
from jax.sharding import PartitionSpec as P

COL = ("col_0", "col_1")
ROW = ("row_0", "row_1", "row_2")
ROW_COL = ("row_0", "row_1", "row_2", "col_0", "col_1")


very_low = -1e30


def sent_together(arrays, axis, dim, along):
    widths = [math.prod(a.shape[along:]) for a in arrays]
    both = jnp.concatenate(
        [a.reshape(*a.shape[:along], w) for a, w in zip(arrays, widths)], axis=along
    )
    out = lax.all_gather(both, axis, axis=dim, tiled=True)
    pieces = jnp.split(out, [sum(widths[:k]) for k in range(1, len(widths))], axis=along)
    return tuple((b.reshape(*out.shape[:along], *a.shape[along:]) for a, b in zip(arrays, pieces)))


def by_axis(value, axes):
    for axis in axes:
        value = lax.psum(value, axis)
    return value


def update(carry, blocks, block_counts, row_stride, queries, positives):
    run_max, run_sum, run_pos = (carry[0], carry[1], carry[2])
    rows, width, feat = blocks.shape
    per = block_counts.shape[1]
    slots = width // per
    grid = blocks.reshape(rows, per, slots, feat)
    scores = jnp.einsum(
        "qd,rkmd->qrkm", queries, grid, preferred_element_type=jnp.float32
    ) * feat ** (-0.5)
    slot = lax.broadcasted_iota(jnp.int32, (rows, per, slots), 2)
    block = lax.broadcasted_iota(jnp.int32, (rows, per, slots), 1)
    line = lax.broadcasted_iota(jnp.int32, (rows, per, slots), 0)
    valid = slot.astype(jnp.float32) < block_counts.astype(jnp.float32)[:, :, None]
    index = line * row_stride + block * slots + slot
    scores = scores.reshape(queries.shape[0], rows * width)
    valid = valid.reshape(-1)
    index = index.reshape(-1)
    masked = jnp.where(valid[None, :], scores, very_low)
    new_max = jnp.maximum(run_max, jnp.max(masked, axis=1))
    new_sum = jnp.sum(jnp.exp(masked - new_max[:, None]), axis=1)
    new_pos = jnp.sum(jnp.where(index[None, :] == positives[:, None], scores, 0.0), axis=1)
    return (new_max, new_sum, new_pos, jnp.sum(block_counts.astype(jnp.float32)))


def shards(queries, documents, counts, positives):
    count_rows = queries.shape[0]
    start_carry = (
        jnp.full((count_rows,), very_low, jnp.float32),
        jnp.zeros((count_rows,), jnp.float32),
        jnp.zeros((count_rows,), jnp.float32),
        jnp.zeros((), jnp.float32),
    )
    small_counts = counts.astype(jnp.bfloat16)
    stride = lax.axis_size(COL) * documents.shape[0]
    gathered, gathered_counts = sent_together((documents[None], small_counts[None]), ROW, 0, 1)
    result = update(
        start_carry,
        lax.all_gather(gathered, COL, axis=1, tiled=True),
        lax.all_gather(gathered_counts, COL, axis=1, tiled=True),
        stride,
        queries,
        positives,
    )
    total = by_axis(jnp.sum(counts.astype(jnp.float32)), ROW_COL)
    lse = result[0] + jnp.log(result[1])
    return lse - result[2] - jnp.log(total)


def solution(mesh):
    finer = Mesh(mesh.devices.reshape(2, 4, 2, 2, 8), ("row_0", "row_1", "row_2", "col_0", "col_1"))
    return jax.shard_map(
        shards,
        mesh=finer,
        in_specs=(P(ROW_COL, None), P(ROW_COL, None), P(ROW_COL), P(ROW_COL)),
        out_specs=P(ROW_COL),
        check_vma=False,
    )
```

profile of v0, /device:TPU:1, one launch (start us, length us, event | category | flops | bytes accessed | tf_op | source)
XLA Modules:
  0.0 260.1 jit_solution(3806381499942437362)
XLA Ops:
  6.5 0.0 copy-start
  6.5 0.0 all-gather.4.cloned.1.call-start
  7.3 0.9 copy.12
  8.2 0.1 maximum_bitcast_fusion
  8.3 25.8 %all-gather = bf16[16,1,24577]{2,1,0:T(2,128)(2,1)S(1)} all-gather(bf16[1,1,24577]{2,1,0:T(2,128)(2,1)S(1)} %maximum_bitcast_fusion), channel_id=1, replica_groups=mesh['row_0'=2,'row_1'=4,'row_2'=2,'col_0'=2,'col_1'=8] {'row_0','row_1'..., dimensions={0}, use_global_device_ids=true | all-gather | bytes 835618 | tf_op jit(solution)/shard_map/all_gather | solution.py:22
  34.2 0.1 copy.15
  34.3 0.1 split.9
  34.3 1.0 copy.13
  35.4 0.0 all-gather.4.cloned.1.call-update
  35.4 4.9 %psum.35 = f32[]{:T(128)} all-reduce(f32[]{:T(128)} %bitcast.8), channel_id=1, replica_groups=mesh['row_0'=2,'row_1'=4,'row_2'=2,'col_0'=2,'col_1'=8] {'row_0'}, use_global_device_ids=true, to_apply=%region_3.4 | all-reduce | flops 1 | bytes 8 | tf_op jit(solution)/shard_map/psum | solution.py:29
  40.3 6.6 %psum.36 = f32[]{:T(128)} all-reduce(f32[]{:T(128)} %psum.35), channel_id=1, replica_groups=mesh['row_0'=2,'row_1'=4,'row_2'=2,'col_0'=2,'col_1'=8] {'row_1'}, use_global_device_ids=true, to_apply=%region_4.5 | all-reduce | flops 1 | bytes 8 | tf_op jit(solution)/shard_map/psum | solution.py:29
  46.9 5.8 %psum.37 = f32[]{:T(128)} all-reduce(f32[]{:T(128)} %psum.36), channel_id=1, replica_groups=mesh['row_0'=2,'row_1'=4,'row_2'=2,'col_0'=2,'col_1'=8] {'row_2'}, use_global_device_ids=true, to_apply=%region_5.6 | all-reduce | flops 1 | bytes 8 | tf_op jit(solution)/shard_map/psum | solution.py:29
  52.7 6.5 %psum.38 = f32[]{:T(128)} all-reduce(f32[]{:T(128)} %psum.37), channel_id=1, replica_groups=mesh['row_0'=2,'row_1'=4,'row_2'=2,'col_0'=2,'col_1'=8] {'col_0'}, use_global_device_ids=true, to_apply=%region_6.7 | all-reduce | flops 1 | bytes 8 | tf_op jit(solution)/shard_map/psum | solution.py:29
  59.2 18.2 %psum.39 = f32[]{:T(128)} all-reduce(f32[]{:T(128)} %psum.38), channel_id=1, replica_groups=mesh['row_0'=2,'row_1'=4,'row_2'=2,'col_0'=2,'col_1'=8] {'col_1'}, use_global_device_ids=true, to_apply=%region_7.8 | all-reduce | flops 1 | bytes 8 | tf_op jit(solution)/shard_map/psum | solution.py:29
  77.3 0.1 slice_reduce_fusion
  77.5 31.0 %all-gather.1 = bf16[16,1,16]{2,1,0:T(2,128)(2,1)S(1)} all-gather(bf16[1,1,16]{2,1,0:T(2,128)(2,1)S(1)} %bitcast.41), channel_id=1, replica_groups=mesh['row_0'=2,'row_1'=4,'row_2'=2,'col_0'=2,'col_1'=8] {'col_0','col_1'}, dimensions={0}, use_global_device_ids=true | all-gather | bytes 544 | tf_op jit(solution)/shard_map/all_gather | solution.py:71
  108.5 0.1 copy.9
  109.3 0.1 broadcast_compare_fusion
  109.4 0.1 iota_add_fusion
  109.5 103.3 %all-gather.4.cloned.1.call-done = bf16[16,512,768]{2,1,0:T(8,128)(2,1)} async-done(((bf16[16,32,768]{2,1,0:T(8,128)(2,1)}), bf16[16,512,768]{2,1,0:T(8,128)(2,1)}) %all-gather.4.cloned.1.call-update) | async-done | bytes 12582928 | tf_op jit(solution)/shard_map/all_gather | solution.py:70
  212.8 0.0 copy-done
  212.8 0.0 copy-start.1
  212.8 23.5 %fusion.1 = (f32[1024]{0:T(1024)S(1)}, f32[16,16,32,1024]{3,2,1,0:T(8,128)}) fusion(pred[16,16,32]{2,1,0:T(8,128)(4,1)S(1)} %broadcast_compare_fusion, bf16[16,16,32,768]{3,2,1,0:T(8,128)(2,1)} %bitcast.42, bf16[1024,768]{1,0:T(8,128)(2,1)S(1)} %copy-done), kind=kOutput, calls=%fused_computation.4 | convolution fusion | flops 12910066688 | bytes 47722496 | tf_op jit(solution)/shard_map/qd,rkmd->qrkm/dot_general | solution.py:39
  236.2 0.0 copy-done.1
  236.2 16.4 %exponential_reduce_fusion = (f32[1024]{0:T(1024)S(1)}, f32[1024]{0:T(1024)S(1)}) fusion(f32[16,16,32,1024]{3,2,1,0:T(8,128)} %get-tuple-element.8, f32[1024]{0:T(1024)S(1)} %broadcast_maximum_fusion, pred[16,16,32]{2,1,0:T(8,128)(4,1)S(1)} %broadcast_compare_fusion, s32[1024]{0:T(1024)S(1)} %copy-done.1, s32[16,16,32]{2,1,0:T(8,128)S(1)} %iota_add_fusion), kind=kLoop, calls=%fused_computation.3 | loop fusion | flops 58718208 | bytes 33611776 | tf_op jit(solution)/shard_map/reduce_sum | solution.py:52
  252.7 0.6 subtract_subtract_fusion
  (4 shorter events, 0.0 us)
Async XLA Ops:
  6.5 206.2 %copy-start = (bf16[1024,768]{1,0:T(8,128)(2,1)S(1)}, bf16[1024,768]{1,0:T(8,128)(2,1)}, u32[]{:S(2)}) copy-start(bf16[1024,768]{1,0:T(8,128)(2,1)} %param.4) | copy-start | bytes 4718596
  6.5 206.2 %all-gather.4.cloned.1.call-start = ((), (), s32[]{:S(2)}) async-start(), calls=%async_computation | async-start | bytes 13369344 | tf_op jit(solution)/shard_map/all_gather | solution.py:70
  212.8 23.5 %copy-start.1 = (s32[1024]{0:T(1024)S(1)}, s32[1024]{0:T(1024)}, u32[]{:S(2)}) copy-start(s32[1024]{0:T(1024)} %param.7) | copy-start | bytes 12292
Sparse Core Ops, SparseCore 0:
  35.5 177.2 all-gather.3
where the time goes:
time: 261 us; the launch traced here: 260 us
  waiting for transfers between devices  103 us (39%)
  blocking collectives  98.8 us (38%)
  matrix products  23.5 us (9%)
  other arithmetic  17.4 us (7%)
  between operations  14.9 us (6%)
    all_gather x1, waiting for transfers between devices, shards(): lax.all_gather(gathered, COL, axis=1, tiled=True)  103 us
    psum x5, blocking collectives, by_axis(): value = lax.psum(value, axis)  41.9 us
    all_gather x1, blocking collectives, shards(): lax.all_gather(gathered_counts, COL, axis=1, tiled=True)  31 us
    all_gather x1, blocking collectives, sent_together(): out = lax.all_gather(both, axis, axis=dim, tiled=True)  25.8 us
    dot_general x1, matrix products, update(): jnp.einsum('qd,rkmd->qrkm', queries, grid, preferred_element_type=jnp.flo...  23.5 us
    reduce_sum x1, other arithmetic, update(): new_sum = jnp.sum(jnp.exp(masked - new_max[:, None]), axis=1)  16.4 us
  transfers between devices with their start and end apart: 1, of which 1 were waited for; matrix products, arithmetic and copies ran while one was open for 0% of the time, Pallas kernels for 0%

commit v1 on v0

v1 whole, which is shorter than its diff:
```python
import functools

import jax
import jax.numpy as jnp
import numpy as np
from jax import lax
from jax.experimental import pallas as pl
from jax.experimental.pallas import tpu as pltpu
from jax.sharding import Mesh
from jax.sharding import PartitionSpec as P

AXES = ("x_lo", "y", "core", "x_hi", "z")
TORUS = (4, 4, 8)
CORES = 2
LOW = -1e30
LOG2E = 1.4426950408889634
TILE_D = 512
TILE_Q = 512
ROUNDS = (
    ((0, 0, 4),),
    ((1, -1, 1), (-1, 1, -1), (2, 2, 2)),
    ((1, 1, 0), (-1, -1, 0), (0, 0, 2)),
    ((1, 0, 0), (0, 1, 0), (0, 0, 1)),
)
LAST_SPLIT = 2


def flat(x, y, z, c):
    return (((x % 2 * 4 + y) * 2 + c) * 2 + x // 2) * 8 + z


def everyone():
    return [(x, y, z, c) for x in range(4) for y in range(4) for z in range(8) for c in range(2)]


def wrap(chip):
    return tuple(int(v) % n for v, n in zip(chip, TORUS))


def by_offset(value, offset):
    pairs = []
    for x, y, z, c in everyone():
        sign = 1 if c == 0 else -1
        to = wrap((x + sign * offset[0], y + sign * offset[1], z + sign * offset[2]))
        pairs.append((flat(x, y, z, c), flat(*to, c)))
    return lax.ppermute(value, AXES, pairs)


def to_partner(value):
    return lax.ppermute(value, "core", [(0, 1), (1, 0)])


def gather(block):
    held, buffer = [(0, 0, 0)], block
    moved = lambda blocks, offset: [wrap(np.subtract(a, offset)) for a in blocks]
    for offsets in ROUNDS[:-1]:
        parts = [by_offset(buffer, o) for o in offsets]
        held = held + [a for o in offsets for a in moved(held, o)]
        buffer = jnp.concatenate([buffer] + parts, axis=0)
    groups, order = [[buffer]], list(held)
    rows, count = buffer.shape[0] // LAST_SPLIT, len(held) // LAST_SPLIT
    for s in range(LAST_SPLIT):
        groups.append([by_offset(buffer[s * rows : (s + 1) * rows], o) for o in ROUNDS[-1]])
        for o in ROUNDS[-1]:
            order += moved(held[s * count : (s + 1) * count], o)
    return groups, order


def first_indices(order, slots):
    x = lax.axis_index("x_hi") * 2 + lax.axis_index("x_lo")
    y, z, c = lax.axis_index("y"), lax.axis_index("z"), lax.axis_index("core")
    sign = 1 - 2 * c
    table = np.asarray(order, np.int32)
    bx = (x + sign * table[:, 0]) % TORUS[0]
    by = (y + sign * table[:, 1]) % TORUS[1]
    bz = (z + sign * table[:, 2]) % TORUS[2]
    return (flat(bx, by, bz, c) * slots).astype(jnp.int32)


def kernel(first, last, block0, slots, scale, n_docs, *refs):
    firsts = refs[0]
    docs = refs[1 : 1 + n_docs]
    queries, wanted = refs[1 + n_docs : 3 + n_docs]
    rest = refs[3 + n_docs :]
    if not first:
        top_in, sum_in, hit_in, count_in = rest[:4]
        rest = rest[4:]
    if last:
        mine, theirs, top, total, hit, count, scores = rest
    else:
        top, total, hit, count, scores = rest
    width = queries.shape[1]
    if first:
        top[...] = jnp.full(top.shape, LOW, jnp.float32)
        total[...] = jnp.zeros(total.shape, jnp.float32)
        hit[...] = jnp.zeros(hit.shape, jnp.float32)
        count[...] = jnp.zeros(count.shape, jnp.float32)
    else:
        top[...] = top_in[...]
        total[...] = sum_in[...]
        hit[...] = hit_in[...]
        count[...] = count_in[...]
    tiles = []
    block = block0
    for ref in docs:
        for row in range(0, ref.shape[0], TILE_D):
            tiles.append((ref, row, block))
            block += TILE_D // slots
    n = len(tiles)
    steps = width // TILE_Q
    factor = scale * LOG2E
    lanes = TILE_Q // 128
    iota = lax.broadcasted_iota(jnp.int32, (8, 128), 0)

    def multiply(j, q):
        ref, row, _ = tiles[j]
        at = pl.multiple_of(q * TILE_Q, TILE_Q)
        scores[j] = jnp.dot(
            ref[row : row + TILE_D, :], queries[:, pl.ds(at, TILE_Q)], preferred_element_type=jnp.float32
        )

    def consume(j, q):
        ref, row, block = tiles[j]
        at = [pl.ds(pl.multiple_of(q * TILE_Q + 128 * l, 128), 128) for l in range(lanes)]
        want = [jnp.broadcast_to(wanted[:, a], (8, 128)) for a in at]
        old = [top[:, a] for a in at]
        new = list(old)
        found = [hit[:, a] for a in at]
        seen = count[...]
        for r in range(0, TILE_D, 16):
            marks = ref[row + r : row + r + 16, 0:128].astype(jnp.float32)
            base = firsts[block + r // slots]
            for h in range(2):
                mark = marks[8 * h : 8 * h + 8]
                valid = mark == mark
                seen = seen + jnp.where(valid, 1.0, 0.0)
                index = iota + (base + (r + 8 * h) % slots)
                for l in range(lanes):
                    part = (j, pl.ds(r + 8 * h, 8), pl.ds(128 * l, 128))
                    s = jnp.where(valid, scores[part], LOW)
                    scores[part] = s
                    new[l] = jnp.maximum(new[l], s)
                    found[l] = jnp.where(index == want[l], s, found[l])
        acc = [total[:, a] * jnp.exp2((o - m) * factor) for a, o, m in zip(at, old, new)]
        for r in range(0, TILE_D, 8):
            for l in range(lanes):
                s = scores[j, pl.ds(r, 8), pl.ds(128 * l, 128)]
                acc[l] = acc[l] + jnp.exp2((s - new[l]) * factor)
        for l in range(lanes):
            top[:, at[l]] = new[l]
            total[:, at[l]] = acc[l]
            hit[:, at[l]] = found[l]
        count[...] = seen

    multiply(0, 0)

    def step(q, carry):
        for j in range(n):
            if j + 1 < n:
                multiply(j + 1, q)
            else:
                multiply(0, jnp.minimum(q + 1, steps - 1))
            consume(j, q)
        return carry

    lax.fori_loop(0, steps, step, 0)
    if last:
        m = jnp.max(top[...], axis=0, keepdims=True)
        s = jnp.sum(total[...] * jnp.exp2((top[...] - m) * factor), axis=0, keepdims=True)
        p = jnp.sum(hit[...], axis=0, keepdims=True)
        seen = jnp.sum(count[...], axis=0, keepdims=True) * (1.0 / steps)
        half = width // 2
        seen = jnp.concatenate([seen] * (half // 128), axis=1)
        for out, a in ((mine, 0), (theirs, half)):
            out[0:1, :] = m[:, a : a + half]
            out[1:2, :] = s[:, a : a + half]
            out[2:3, :] = p[:, a : a + half]
            out[3:4, :] = seen


def chunk(docs, firsts, queries, wanted, carry, last, block0, slots, scale):
    width = queries.shape[1]
    state = [jax.ShapeDtypeStruct((8, width), jnp.float32)] * 3 + [jax.ShapeDtypeStruct((8, 128), jnp.float32)]
    vmem = pl.BlockSpec(memory_space=pltpu.VMEM)
    n = sum(d.shape[0] for d in docs)
    scratch = [pltpu.VMEM((n // TILE_D, TILE_D, TILE_Q), jnp.float32)]
    if last:
        out = [jax.ShapeDtypeStruct((4, width // 2), jnp.float32)] * 2
        scratch = [pltpu.VMEM(s.shape, s.dtype) for s in state] + scratch
    else:
        out = state
    given = [*docs, queries, wanted, *(carry or ())]
    return pl.pallas_call(
        functools.partial(kernel, carry is None, last, block0, slots, scale, len(docs)),
        out_shape=out,
        in_specs=[pl.BlockSpec(memory_space=pltpu.SMEM)] + [vmem] * len(given),
        out_specs=[vmem] * len(out),
        scratch_shapes=scratch,
        cost_estimate=pl.CostEstimate(
            flops=2 * n * width * queries.shape[0], bytes_accessed=2 * n * queries.shape[0], transcendentals=n * width
        ),
        compiler_params=pltpu.CompilerParams(vmem_limit_bytes=24 * 1024 * 1024),
    )(firsts, *given)


def shards(queries, documents, counts, positives):
    slots, feat = documents.shape
    scale = feat ** (-0.5)
    slot = lax.broadcasted_iota(jnp.int32, documents.shape, 0)
    marked = jnp.where(slot < counts[0], documents, jnp.bfloat16(jnp.nan))
    groups, order = gather(marked)
    both = jnp.concatenate([queries, to_partner(queries)], axis=0).T
    wanted = positives[None, :]
    wanted = jnp.concatenate([wanted, to_partner(wanted)], axis=1)
    firsts = first_indices(order, slots)
    carry, block = None, 0
    for k, docs in enumerate(groups):
        carry = chunk(docs, firsts, both, wanted, carry, k == len(groups) - 1, block, slots, scale)
        block += sum(d.shape[0] for d in docs) // slots
    mine, theirs = carry
    other = to_partner(theirs)
    top = jnp.maximum(mine[0], other[0])
    total = mine[1] * jnp.exp((mine[0] - top) * scale) + other[1] * jnp.exp((other[0] - top) * scale)
    lse = top * scale + jnp.log(total)
    return lse - (mine[2] + other[2]) * scale - jnp.log(mine[3] + other[3])


def solution(mesh):
    finer = Mesh(mesh.devices.reshape(2, 4, 2, 2, 8), AXES)
    return jax.shard_map(
        shards,
        mesh=finer,
        in_specs=(P(AXES, None), P(AXES, None), P(AXES), P(AXES)),
        out_specs=P(AXES),
        check_vma=False,
    )
```

time: 261 us -> 95 us (0.36)
  blocking collectives: 98.8 us -> 0 us
  waiting for transfers between devices: 103 us -> 20.7 us
  starting transfers between devices: 0.01 us -> 43.8 us
  matrix products: 23.5 us -> 0 us
  Pallas kernels: 0 us -> 22.3 us
  between operations: 14.9 us -> 0.81 us
  other arithmetic: 17.4 us -> 3.67 us
    all_gather x1 -> x0, waiting for transfers between devices: 103 us -> none  [shards(): lax.all_gather(gathered, COL, axis=1, tiled=True)]
    all_gather x2 -> x0, blocking collectives: 56.9 us -> none  [the longest x1 31 us: shards(): lax.all_gather(gathered_counts, COL, axis=1, tiled=True)]
    ppermute x0 -> x16, starting transfers between devices: none -> 43.8 us  [the longest x13 36.3 us: by_offset(): return lax.ppermute(value, AXES, pairs)]
    psum x5 -> x0, blocking collectives: 41.9 us -> none  [by_axis(): value = lax.psum(value, axis)]
    dot_general x1 -> x0, matrix products: 23.5 us -> none  [update(): jnp.einsum('qd,rkmd->qrkm', queries, grid, preferred_element_type=jnp.flo...]
    pallas_call x0 -> x3, Pallas kernels: none -> 22.3 us  [chunk(): pl.pallas_call(functools.partial(kernel, carry is None, last, block0, slo...]
    ppermute x0 -> x16, waiting for transfers between devices: none -> 20.7 us  [the longest x13 19.9 us: by_offset(): return lax.ppermute(value, AXES, pairs)]
    reduce_sum x1 -> x0, other arithmetic: 16.4 us -> none  [update(): new_sum = jnp.sum(jnp.exp(masked - new_max[:, None]), axis=1)]
  transfers between devices with their start and end apart: 1 -> 16, of which waited for: 1 -> 6; matrix products, arithmetic and copies ran while one was open for 0% -> 3% of each run, Pallas kernels for 0% -> 15%
where the time goes in v1:
time: 95 us; the launch traced here: 94.2 us
  starting transfers between devices  43.8 us (46%)
  Pallas kernels  22.3 us (23%)
  waiting for transfers between devices  20.7 us (22%)
  other arithmetic  3.67 us (4%)
  local copies, waits for them, and re-layouts  2.89 us (3%)
    ppermute x13, starting transfers between devices, by_offset(): return lax.ppermute(value, AXES, pairs)  36.3 us
    pallas_call x3, Pallas kernels, chunk(): pl.pallas_call(functools.partial(kernel, carry is None, last, block0, slo...  22.3 us
    ppermute x13, waiting for transfers between devices, by_offset(): return lax.ppermute(value, AXES, pairs)  19.9 us
    ppermute x3, starting transfers between devices, to_partner(): return lax.ppermute(value, 'core', [(0, 1), (1, 0)])  7.49 us
    unnamed x16, local copies, waits for them, and re-layouts  2.84 us
    transpose x1, other arithmetic, shards(): both = jnp.concatenate([queries, to_partner(queries)], axis=0).T  2.24 us
  transfers between devices with their start and end apart: 16, of which 6 were waited for; matrix products, arithmetic and copies ran while one was open for 3% of the time, Pallas kernels for 15%

profile of v1, /device:TPU:1, one launch (start us, length us, event | category | flops | bytes accessed | tf_op | source)
XLA Modules:
  0.0 94.2 jit_solution(14564952277768523745)
XLA Ops:
  0.0 0.0 copy-start
  0.0 2.6 %copy.9 = bf16[1024,768]{0,1:T(8,128)(2,1)} copy(bf16[1024,768]{1,0:T(8,128)(2,1)} %param.7) | data formatting | bytes 3145728 | tf_op args[0]
  2.6 3.3 %collective-permute-start.9 = (bf16[1024,768]{0,1:T(8,128)(2,1)}, bf16[1024,768]{0,1:T(8,128)(2,1)}, u32[]{:S(2)}, u32[]{:S(2)}) collective-permute-start(bf16[1024,768]{0,1:T(8,128)(2,1)} %copy.9), channel_id=1, source_target_pairs={{0,16},{16,0},{1,17},{17,1},{2,18},{18,2},{3,19},{19,3},{4,20},{20... | collective-permute-start | bytes 4718600 | tf_op jit(solution)/shard_map/ppermute | solution.py:50
  6.6 0.0 copy-done
  6.6 0.1 constant_dynamic-update-slice_fusion.20
  6.7 5.3 %collective-permute-start = (bf16[32,768]{1,0:T(8,128)(2,1)S(1)}, bf16[32,768]{1,0:T(8,128)(2,1)S(1)}, u32[]{:S(2)}, u32[]{:S(2)}) collective-permute-start(bf16[32,768]{1,0:T(8,128)(2,1)S(1)} %get-tuple-element.26), channel_id=1, source_target_pairs={{0,4},{16,20},{1,5},{17,21},{2,6},{18,22},{3,7},{19,23},{4,0},{20,... | collective-permute-start | bytes 147464 | tf_op jit(solution)/shard_map/ppermute | solution.py:46
  12.0 2.0 %collective-permute-done = bf16[32,768]{1,0:T(8,128)(2,1)S(1)} collective-permute-done((bf16[32,768]{1,0:T(8,128)(2,1)S(1)}, bf16[32,768]{1,0:T(8,128)(2,1)S(1)}, u32[]{:S(2)}, u32[]{:S(2)}) %collective-permute-start) | collective-permute-done | bytes 49184 | tf_op jit(solution)/shard_map/ppermute | solution.py:46
  14.0 9.5 %collective-permute-start.3 = (bf16[64,768]{1,0:T(8,128)(2,1)S(1)}, bf16[64,768]{1,0:T(8,128)(2,1)S(1)}, u32[]{:S(2)}, u32[]{:S(2)}) collective-permute-start(bf16[64,768]{1,0:T(8,128)(2,1)S(1)} %pad_maximum_fusion), channel_id=1, source_target_pairs={{0,74},{16,94},{1,75},{17,95},{2,76},{18,88},{3,77},{19,89},{4,78}... | collective-permute-start | bytes 294920 | tf_op jit(solution)/shard_map/ppermute | solution.py:46
  23.4 1.3 %collective-permute-start.2 = (bf16[64,768]{1,0:T(8,128)(2,1)S(1)}, bf16[64,768]{1,0:T(8,128)(2,1)S(1)}, u32[]{:S(2)}, u32[]{:S(2)}) collective-permute-start(bf16[64,768]{1,0:T(8,128)(2,1)S(1)} %pad_maximum_fusion), channel_id=1, source_target_pairs={{0,175},{16,241},{1,168},{17,242},{2,169},{18,243},{3,170},{19,244... | collective-permute-start | bytes 294920 | tf_op jit(solution)/shard_map/ppermute | solution.py:46
  24.7 4.4 %collective-permute-start.1 = (bf16[64,768]{1,0:T(8,128)(2,1)S(1)}, bf16[64,768]{1,0:T(8,128)(2,1)S(1)}, u32[]{:S(2)}, u32[]{:S(2)}) collective-permute-start(bf16[64,768]{1,0:T(8,128)(2,1)S(1)} %pad_maximum_fusion), channel_id=1, source_target_pairs={{0,225},{16,191},{1,226},{17,184},{2,227},{18,185},{3,228},{19,186... | collective-permute-start | bytes 294920 | tf_op jit(solution)/shard_map/ppermute | solution.py:46
  29.1 2.0 %collective-permute-done.1 = bf16[64,768]{1,0:T(8,128)(2,1)S(1)} collective-permute-done((bf16[64,768]{1,0:T(8,128)(2,1)S(1)}, bf16[64,768]{1,0:T(8,128)(2,1)S(1)}, u32[]{:S(2)}, u32[]{:S(2)}) %collective-permute-start.1) | collective-permute-done | bytes 98336 | tf_op jit(solution)/shard_map/ppermute | solution.py:46
  31.2 0.0 collective-permute-done.2
  31.2 0.0 collective-permute-done.3
  31.3 1.7 %collective-permute-start.11 = (bf16[256,768]{1,0:T(8,128)(2,1)S(1)}, bf16[256,768]{1,0:T(8,128)(2,1)S(1)}, u32[]{:S(2)}, u32[]{:S(2)}) collective-permute-start(bf16[256,768]{1,0:T(8,128)(2,1)S(1)} %get-tuple-element.35), channel_id=1, source_target_pairs={{0,160},{16,248},{1,161},{17,249},{2,162},{18,250},{3,163},{19,251... | collective-permute-start | bytes 1179656 | tf_op jit(solution)/shard_map/ppermute | solution.py:46
  33.0 5.9 %collective-permute-done.11 = bf16[256,768]{1,0:T(8,128)(2,1)S(1)} collective-permute-done((bf16[256,768]{1,0:T(8,128)(2,1)S(1)}, bf16[256,768]{1,0:T(8,128)(2,1)S(1)}, u32[]{:S(2)}, u32[]{:S(2)}) %collective-permute-start.11) | collective-permute-done | bytes 393248 | tf_op jit(solution)/shard_map/ppermute | solution.py:46
  38.9 0.1 constant_dynamic-update-slice_fusion.15
  38.9 3.5 %collective-permute-start.14 = (bf16[512,768]{1,0:T(8,128)(2,1)S(1)}, bf16[512,768]{1,0:T(8,128)(2,1)S(1)}, u32[]{:S(2)}, u32[]{:S(2)}) collective-permute-start(bf16[512,768]{1,0:T(8,128)(2,1)S(1)} %get-tuple-element.32), channel_id=1, source_target_pairs={{0,1},{16,23},{1,2},{17,16},{2,3},{18,17},{3,4},{19,18},{4,5},{20,... | collective-permute-start | bytes 2359304 | tf_op jit(solution)/shard_map/ppermute | solution.py:46
  42.5 0.0 copy-done.1
  42.5 2.1 %collective-permute-start.10 = (s32[1,1024]{1,0:T(1,128)S(1)}, s32[1,1024]{1,0:T(1,128)S(1)}, u32[]{:S(2)}, u32[]{:S(2)}) collective-permute-start(s32[1,1024]{1,0:T(1,128)S(1)} %bitcast.17), channel_id=1, source_target_pairs={{0,16},{16,0},{1,17},{17,1},{2,18},{18,2},{3,19},{19,3},{4,20},{20... | collective-permute-start | bytes 12296 | tf_op jit(solution)/shard_map/ppermute | solution.py:50
  44.6 2.2 %collective-permute-start.5 = (bf16[256,768]{1,0:T(8,128)(2,1)S(1)}, bf16[256,768]{1,0:T(8,128)(2,1)S(1)}, u32[]{:S(2)}, u32[]{:S(2)}) collective-permute-start(bf16[256,768]{1,0:T(8,128)(2,1)S(1)} %get-tuple-element.35), channel_id=1, source_target_pairs={{0,2},{16,22},{1,3},{17,23},{2,4},{18,16},{3,5},{19,17},{4,6},{20,... | collective-permute-start | bytes 1179656 | tf_op jit(solution)/shard_map/ppermute | solution.py:46
  46.7 0.0 collective-permute-start.4
  46.7 0.0 copy-done.2
  46.7 0.0 copy-done.3
  46.7 0.7 fusion.8.refs_0_
  47.4 0.0 collective-permute-done.10
  47.4 2.4 %collective-permute-start.13 = (bf16[512,768]{1,0:T(8,128)(2,1)S(1)}, bf16[512,768]{1,0:T(8,128)(2,1)S(1)}, u32[]{:S(2)}, u32[]{:S(2)}) collective-permute-start(bf16[512,768]{1,0:T(8,128)(2,1)S(1)} %get-tuple-element.32), channel_id=1, source_target_pairs={{0,32},{16,112},{1,33},{17,113},{2,34},{18,114},{3,35},{19,115},{4... | collective-permute-start | bytes 2359304 | tf_op jit(solution)/shard_map/ppermute | solution.py:46
  49.8 7.0 %collective-permute-done.4 = bf16[256,768]{1,0:T(8,128)(2,1)S(1)} collective-permute-done((bf16[256,768]{1,0:T(8,128)(2,1)S(1)}, bf16[256,768]{1,0:T(8,128)(2,1)S(1)}, u32[]{:S(2)}, u32[]{:S(2)}) %collective-permute-start.4) | collective-permute-done | bytes 393248 | tf_op jit(solution)/shard_map/ppermute | solution.py:46
  56.8 0.0 collective-permute-start.12
  56.8 0.1 constant_dynamic-update-slice_fusion.14
  56.8 3.0 %collective-permute-done.5 = bf16[256,768]{1,0:T(8,128)(2,1)S(1)} collective-permute-done((bf16[256,768]{1,0:T(8,128)(2,1)S(1)}, bf16[256,768]{1,0:T(8,128)(2,1)S(1)}, u32[]{:S(2)}, u32[]{:S(2)}) %collective-permute-start.5) | collective-permute-done | bytes 393248 | tf_op jit(solution)/shard_map/ppermute | solution.py:46
  59.8 0.1 constant_dynamic-update-slice_fusion.13
  59.9 1.0 %collective-permute-start.8 = (bf16[512,768]{1,0:T(8,128)(2,1)S(1)}, bf16[512,768]{1,0:T(8,128)(2,1)S(1)}, u32[]{:S(2)}, u32[]{:S(2)}) collective-permute-start(bf16[512,768]{1,0:T(8,128)(2,1)S(1)} %get-tuple-element.28), channel_id=1, source_target_pairs={{0,1},{16,23},{1,2},{17,16},{2,3},{18,17},{3,4},{19,18},{4,5},{20,... | collective-permute-start | bytes 2359304 | tf_op jit(solution)/shard_map/ppermute | solution.py:46
  60.9 0.0 collective-permute-done.14.refs_3_
  60.9 3.3 %collective-permute-start.7 = (bf16[512,768]{1,0:T(8,128)(2,1)S(1)}, bf16[512,768]{1,0:T(8,128)(2,1)S(1)}, u32[]{:S(2)}, u32[]{:S(2)}) collective-permute-start(bf16[512,768]{1,0:T(8,128)(2,1)S(1)} %get-tuple-element.28), channel_id=1, source_target_pairs={{0,32},{16,112},{1,33},{17,113},{2,34},{18,114},{3,35},{19,115},{4... | collective-permute-start | bytes 2359304 | tf_op jit(solution)/shard_map/ppermute | solution.py:46
  64.2 0.0 collective-permute-done.9
  64.2 1.8 %collective-permute-start.6 = (bf16[512,768]{1,0:T(8,128)(2,1)S(1)}, bf16[512,768]{1,0:T(8,128)(2,1)S(1)}, u32[]{:S(2)}, u32[]{:S(2)}) collective-permute-start(bf16[512,768]{1,0:T(8,128)(2,1)S(1)} %get-tuple-element.28), channel_id=1, source_target_pairs={{0,128},{16,152},{1,129},{17,153},{2,130},{18,154},{3,131},{19,155... | collective-permute-start | bytes 2359304 | tf_op jit(solution)/shard_map/ppermute | solution.py:46
  66.0 2.2 %maximum_bitcast_fusion.refs_2_.refs_4_ = bf16[768,2048]{1,0:T(8,128)(2,1)S(1)} fusion(bf16[1024,768]{0,1:T(8,128)(2,1)} %collective-permute-done.9, bf16[1024,768]{0,1:T(8,128)(2,1)} %copy.9), kind=kLoop, calls=%fused_computation | loop fusion | flops 6291456 | bytes 6291456 | tf_op jit(solution)/shard_map/transpose | solution.py:212
  68.2 5.8 %shard_map.73 = (f32[8,2048]{1,0:T(8,128)S(1)}, f32[8,2048]{1,0:T(8,128)S(1)}, f32[8,2048]{1,0:T(8,128)S(1)}, f32[8,128]{1,0:T(8,128)S(1)}) custom-call(s32[128]{0:T(128)S(1)} %fusion.8.refs_0_, bf16[1024,768]{1,0:T(8,128)(2,1)S(1)} %get-tuple-element.27.refs_1_, bf16[768,2048]{1,0:T(8,128)(2,1)S(1)} %maximum_bitcast_fusion.refs_2_.refs_4_, ...), custom_call_target="tpu_custom_call" | custom-call | flops 3221225472 | bytes 1572864 | tf_op jit(solution)/shard_map/pallas_call | solution.py:193
  74.0 0.0 collective-permute-done.13.refs_2_
  74.0 0.0 collective-permute-done.12.refs_1_
  74.0 8.2 %shard_map.74 = (f32[8,2048]{1,0:T(8,128)S(1)}, f32[8,2048]{1,0:T(8,128)S(1)}, f32[8,2048]{1,0:T(8,128)S(1)}, f32[8,128]{1,0:T(8,128)S(1)}) custom-call(s32[128]{0:T(128)S(1)} %fusion.8.refs_0_, bf16[512,768]{1,0:T(8,128)(2,1)S(1)} %collective-permute-done.12.refs_1_, bf16[512,768]{1,0:T(8,128)(2,1)S(1)} %collective-permute-done.13.refs_2_, ...), custom_call_target="tpu_custom_call" | custom-call | flops 4831838208 | bytes 2359296 | tf_op jit(solution)/shard_map/pallas_call | solution.py:193
  82.3 0.0 collective-permute-done.8.refs_3_
  82.3 0.0 collective-permute-done.7.refs_2_
  82.3 0.0 collective-permute-done.6.refs_1_
  82.3 8.3 %shard_map.75 = (f32[4,1024]{1,0:T(4,128)S(1)}, f32[4,1024]{1,0:T(4,128)S(1)}) custom-call(s32[128]{0:T(128)S(1)} %fusion.8.refs_0_, bf16[512,768]{1,0:T(8,128)(2,1)S(1)} %collective-permute-done.6.refs_1_, bf16[512,768]{1,0:T(8,128)(2,1)S(1)} %collective-permute-done.7.refs_2_, bf16[512,768]{1,0:T(8,128)(2,1)S(1)} %collective-permute-done.8.refs_3_, ...), custom_call_target="tpu_custom_call" | custom-call | flops 4831838208 | bytes 2359296 | tf_op jit(solution)/shard_map/pallas_call | solution.py:193
  90.6 2.1 %collective-permute-start.15 = (f32[4,1024]{1,0:T(4,128)S(1)}, f32[4,1024]{1,0:T(4,128)S(1)}, u32[]{:S(2)}, u32[]{:S(2)}) collective-permute-start(f32[4,1024]{1,0:T(4,128)S(1)} %get-tuple-element.24), channel_id=1, source_target_pairs={{0,16},{16,0},{1,17},{17,1},{2,18},{18,2},{3,19},{19,3},{4,20},{20... | collective-permute-start | bytes 49160 | tf_op jit(solution)/shard_map/ppermute | solution.py:50
  92.7 0.8 collective-permute-done.15
  93.6 0.6 subtract_subtract_fusion
  (12 shorter events, 0.1 us)
Async XLA Ops:
  0.0 6.6 %copy-start = (bf16[32,768]{1,0:T(8,128)(2,1)S(1)}, bf16[32,768]{1,0:T(8,128)(2,1)}, u32[]{:S(2)}) copy-start(bf16[32,768]{1,0:T(8,128)(2,1)} %param.8) | copy-start | bytes 147460
  2.6 39.8 %copy-start.1 = (s32[1024]{0:T(1024)S(1)}, s32[1024]{0:T(1024)}, u32[]{:S(2)}) copy-start(s32[1024]{0:T(1024)} %param.10) | copy-start | bytes 12292
  2.6 44.1 %copy-start.2 = (s32[128]{0:T(128)S(1)}, s32[128]{0:T(128)}, u32[]{:S(2)}) copy-start(s32[128]{0:T(128)} %constant.92.clone) | copy-start | bytes 1540
  2.6 44.1 %copy-start.3 = (s32[128]{0:T(128)S(1)}, s32[128]{0:T(128)}, u32[]{:S(2)}) copy-start(s32[128]{0:T(128)} %constant.91.clone) | copy-start | bytes 1540
  2.6 61.6 %collective-permute-start.9 = (bf16[1024,768]{0,1:T(8,128)(2,1)}, bf16[1024,768]{0,1:T(8,128)(2,1)}, u32[]{:S(2)}, u32[]{:S(2)}) collective-permute-start(bf16[1024,768]{0,1:T(8,128)(2,1)} %copy.9), channel_id=1, source_target_pairs={{0,16},{16,0},{1,17},{17,1},{2,18},{18,2},{3,19},{19,3},{4,20},{20... | collective-permute-start | bytes 4718600 | tf_op jit(solution)/shard_map/ppermute | solution.py:50
  6.7 7.3 %collective-permute-start = (bf16[32,768]{1,0:T(8,128)(2,1)S(1)}, bf16[32,768]{1,0:T(8,128)(2,1)S(1)}, u32[]{:S(2)}, u32[]{:S(2)}) collective-permute-start(bf16[32,768]{1,0:T(8,128)(2,1)S(1)} %get-tuple-element.26), channel_id=1, source_target_pairs={{0,4},{16,20},{1,5},{17,21},{2,6},{18,22},{3,7},{19,23},{4,0},{20,... | collective-permute-start | bytes 147464 | tf_op jit(solution)/shard_map/ppermute | solution.py:46
  14.0 17.3 %collective-permute-start.3 = (bf16[64,768]{1,0:T(8,128)(2,1)S(1)}, bf16[64,768]{1,0:T(8,128)(2,1)S(1)}, u32[]{:S(2)}, u32[]{:S(2)}) collective-permute-start(bf16[64,768]{1,0:T(8,128)(2,1)S(1)} %pad_maximum_fusion), channel_id=1, source_target_pairs={{0,74},{16,94},{1,75},{17,95},{2,76},{18,88},{3,77},{19,89},{4,78}... | collective-permute-start | bytes 294920 | tf_op jit(solution)/shard_map/ppermute | solution.py:46
  23.4 7.8 %collective-permute-start.2 = (bf16[64,768]{1,0:T(8,128)(2,1)S(1)}, bf16[64,768]{1,0:T(8,128)(2,1)S(1)}, u32[]{:S(2)}, u32[]{:S(2)}) collective-permute-start(bf16[64,768]{1,0:T(8,128)(2,1)S(1)} %pad_maximum_fusion), channel_id=1, source_target_pairs={{0,175},{16,241},{1,168},{17,242},{2,169},{18,243},{3,170},{19,244... | collective-permute-start | bytes 294920 | tf_op jit(solution)/shard_map/ppermute | solution.py:46
  24.7 6.5 %collective-permute-start.1 = (bf16[64,768]{1,0:T(8,128)(2,1)S(1)}, bf16[64,768]{1,0:T(8,128)(2,1)S(1)}, u32[]{:S(2)}, u32[]{:S(2)}) collective-permute-start(bf16[64,768]{1,0:T(8,128)(2,1)S(1)} %pad_maximum_fusion), channel_id=1, source_target_pairs={{0,225},{16,191},{1,226},{17,184},{2,227},{18,185},{3,228},{19,186... | collective-permute-start | bytes 294920 | tf_op jit(solution)/shard_map/ppermute | solution.py:46
  31.3 7.6 %collective-permute-start.11 = (bf16[256,768]{1,0:T(8,128)(2,1)S(1)}, bf16[256,768]{1,0:T(8,128)(2,1)S(1)}, u32[]{:S(2)}, u32[]{:S(2)}) collective-permute-start(bf16[256,768]{1,0:T(8,128)(2,1)S(1)} %get-tuple-element.35), channel_id=1, source_target_pairs={{0,160},{16,248},{1,161},{17,249},{2,162},{18,250},{3,163},{19,251... | collective-permute-start | bytes 1179656 | tf_op jit(solution)/shard_map/ppermute | solution.py:46
  38.9 22.0 %collective-permute-start.14 = (bf16[512,768]{1,0:T(8,128)(2,1)S(1)}, bf16[512,768]{1,0:T(8,128)(2,1)S(1)}, u32[]{:S(2)}, u32[]{:S(2)}) collective-permute-start(bf16[512,768]{1,0:T(8,128)(2,1)S(1)} %get-tuple-element.32), channel_id=1, source_target_pairs={{0,1},{16,23},{1,2},{17,16},{2,3},{18,17},{3,4},{19,18},{4,5},{20,... | collective-permute-start | bytes 2359304 | tf_op jit(solution)/shard_map/ppermute | solution.py:46
  42.5 5.0 %collective-permute-start.10 = (s32[1,1024]{1,0:T(1,128)S(1)}, s32[1,1024]{1,0:T(1,128)S(1)}, u32[]{:S(2)}, u32[]{:S(2)}) collective-permute-start(s32[1,1024]{1,0:T(1,128)S(1)} %bitcast.17), channel_id=1, source_target_pairs={{0,16},{16,0},{1,17},{17,1},{2,18},{18,2},{3,19},{19,3},{4,20},{20... | collective-permute-start | bytes 12296 | tf_op jit(solution)/shard_map/ppermute | solution.py:50
  44.6 15.2 %collective-permute-start.5 = (bf16[256,768]{1,0:T(8,128)(2,1)S(1)}, bf16[256,768]{1,0:T(8,128)(2,1)S(1)}, u32[]{:S(2)}, u32[]{:S(2)}) collective-permute-start(bf16[256,768]{1,0:T(8,128)(2,1)S(1)} %get-tuple-element.35), channel_id=1, source_target_pairs={{0,2},{16,22},{1,3},{17,23},{2,4},{18,16},{3,5},{19,17},{4,6},{20,... | collective-permute-start | bytes 1179656 | tf_op jit(solution)/shard_map/ppermute | solution.py:46
  46.7 10.0 %collective-permute-start.4 = (bf16[256,768]{1,0:T(8,128)(2,1)S(1)}, bf16[256,768]{1,0:T(8,128)(2,1)S(1)}, u32[]{:S(2)}, u32[]{:S(2)}) collective-permute-start(bf16[256,768]{1,0:T(8,128)(2,1)S(1)} %get-tuple-element.35), channel_id=1, source_target_pairs={{0,232},{16,176},{1,233},{17,177},{2,234},{18,178},{3,235},{19,179... | collective-permute-start | bytes 1179656 | tf_op jit(solution)/shard_map/ppermute | solution.py:46
  47.4 26.6 %collective-permute-start.13 = (bf16[512,768]{1,0:T(8,128)(2,1)S(1)}, bf16[512,768]{1,0:T(8,128)(2,1)S(1)}, u32[]{:S(2)}, u32[]{:S(2)}) collective-permute-start(bf16[512,768]{1,0:T(8,128)(2,1)S(1)} %get-tuple-element.32), channel_id=1, source_target_pairs={{0,32},{16,112},{1,33},{17,113},{2,34},{18,114},{3,35},{19,115},{4... | collective-permute-start | bytes 2359304 | tf_op jit(solution)/shard_map/ppermute | solution.py:46
  56.8 17.3 %collective-permute-start.12 = (bf16[512,768]{1,0:T(8,128)(2,1)S(1)}, bf16[512,768]{1,0:T(8,128)(2,1)S(1)}, u32[]{:S(2)}, u32[]{:S(2)}) collective-permute-start(bf16[512,768]{1,0:T(8,128)(2,1)S(1)} %get-tuple-element.32), channel_id=1, source_target_pairs={{0,128},{16,152},{1,129},{17,153},{2,130},{18,154},{3,131},{19,155... | collective-permute-start | bytes 2359304 | tf_op jit(solution)/shard_map/ppermute | solution.py:46
  59.9 22.4 %collective-permute-start.8 = (bf16[512,768]{1,0:T(8,128)(2,1)S(1)}, bf16[512,768]{1,0:T(8,128)(2,1)S(1)}, u32[]{:S(2)}, u32[]{:S(2)}) collective-permute-start(bf16[512,768]{1,0:T(8,128)(2,1)S(1)} %get-tuple-element.28), channel_id=1, source_target_pairs={{0,1},{16,23},{1,2},{17,16},{2,3},{18,17},{3,4},{19,18},{4,5},{20,... | collective-permute-start | bytes 2359304 | tf_op jit(solution)/shard_map/ppermute | solution.py:46
  60.9 21.4 %collective-permute-start.7 = (bf16[512,768]{1,0:T(8,128)(2,1)S(1)}, bf16[512,768]{1,0:T(8,128)(2,1)S(1)}, u32[]{:S(2)}, u32[]{:S(2)}) collective-permute-start(bf16[512,768]{1,0:T(8,128)(2,1)S(1)} %get-tuple-element.28), channel_id=1, source_target_pairs={{0,32},{16,112},{1,33},{17,113},{2,34},{18,114},{3,35},{19,115},{4... | collective-permute-start | bytes 2359304 | tf_op jit(solution)/shard_map/ppermute | solution.py:46
  64.2 18.1 %collective-permute-start.6 = (bf16[512,768]{1,0:T(8,128)(2,1)S(1)}, bf16[512,768]{1,0:T(8,128)(2,1)S(1)}, u32[]{:S(2)}, u32[]{:S(2)}) collective-permute-start(bf16[512,768]{1,0:T(8,128)(2,1)S(1)} %get-tuple-element.28), channel_id=1, source_target_pairs={{0,128},{16,152},{1,129},{17,153},{2,130},{18,154},{3,131},{19,155... | collective-permute-start | bytes 2359304 | tf_op jit(solution)/shard_map/ppermute | solution.py:46
  90.6 2.9 %collective-permute-start.15 = (f32[4,1024]{1,0:T(4,128)S(1)}, f32[4,1024]{1,0:T(4,128)S(1)}, u32[]{:S(2)}, u32[]{:S(2)}) collective-permute-start(f32[4,1024]{1,0:T(4,128)S(1)} %get-tuple-element.24), channel_id=1, source_target_pairs={{0,16},{16,0},{1,17},{17,1},{2,18},{18,2},{3,19},{19,3},{4,20},{20... | collective-permute-start | bytes 49160 | tf_op jit(solution)/shard_map/ppermute | solution.py:50

commit v2 on v0

v2 whole, which is shorter than its diff:
```python
import functools

import jax
import jax.numpy as jnp
import numpy as np
from jax import lax
from jax.experimental import pallas as pl
from jax.experimental.pallas import tpu as pltpu
from jax.sharding import Mesh
from jax.sharding import PartitionSpec as P


AXES = ("x_lo", "y", "core", "x_hi", "z")
TORUS = (4, 4, 8)
LOW = -1e30
LOG2E = 1.4426950408889634
TILE_Q = 512
LANES = 128
EXTRA = 16
PIECES = 1
AHEAD = 3
UNROLL = 2
VMEM_LIMIT = 60 * 1024 * 1024
NEAR = (((0, 0, 4),), ((2, 2, 2), (-1, 1, -1), (1, -1, 1)))
FAR = ((1, 1, 0), (-1, -1, 0), (0, 0, 2))
NEIGHBOURS = ((1, 0, 0), (0, 1, 0), (0, 0, 1))


def flat(x, y, z, c):
    return (((x % 2 * 4 + y) * 2 + c) * 2 + x // 2) * 8 + z


def wrap(chip):
    return tuple(int(v) % n for v, n in zip(chip, TORUS))


def by_offset(value, offset):
    pairs = []
    for x in range(4):
        for y in range(4):
            for z in range(8):
                for c in range(2):
                    sign = 1 - 2 * c
                    to = wrap((x + sign * offset[0], y + sign * offset[1], z + sign * offset[2]))
                    pairs.append((flat(x, y, z, c), flat(*to, c)))
    return lax.ppermute(value, AXES, pairs)


def to_partner(value):
    return lax.ppermute(value, "core", [(0, 1), (1, 0)])


def moved(blocks, offset):
    return [wrap(np.subtract(a, offset)) for a in blocks]


def first_indices(parts, slots):
    x = lax.axis_index("x_hi") * 2 + lax.axis_index("x_lo")
    y, z, c = lax.axis_index("y"), lax.axis_index("z"), lax.axis_index("core")
    table = np.concatenate([np.asarray(p + p, np.int32) for p in parts])
    other = np.concatenate([np.repeat(np.int32([0, 1]), len(p)) for p in parts])
    core = (c + other) % 2
    sign = 1 - 2 * core
    bx = (x + sign * table[:, 0]) % TORUS[0]
    by = (y + sign * table[:, 1]) % TORUS[1]
    bz = (z + sign * table[:, 2]) % TORUS[2]
    return (flat(bx, by, bz, core) * slots).astype(jnp.int32)


def prepare(queries_ref, wanted_ref, *out_refs):
    rows, feat = queries_ref.shape
    wanted = wanted_ref[...]
    high = (wanted // LANES).astype(jnp.float32)
    low = (wanted % LANES).astype(jnp.float32)
    row = lax.broadcasted_iota(jnp.int32, (EXTRA, rows), 0)
    codes = jnp.where(row == 0, high, jnp.where(row == 1, low, 0.0)).astype(queries_ref.dtype)
    for k, out in enumerate(out_refs):
        at = slice(k * TILE_Q, (k + 1) * TILE_Q)
        out[0:feat, :] = queries_ref[at, :].T
        out[feat : feat + EXTRA, :] = codes[:, at]


def prepared(queries, positives):
    rows, feat = queries.shape
    vmem = pl.BlockSpec(memory_space=pltpu.VMEM)
    tiles = rows // TILE_Q
    return pl.pallas_call(
        prepare,
        out_shape=[jax.ShapeDtypeStruct((feat + EXTRA, TILE_Q), queries.dtype)] * tiles,
        in_specs=[vmem] * 2,
        out_specs=[vmem] * tiles,
        cost_estimate=pl.CostEstimate(flops=2**26, bytes_accessed=4 * rows * feat, transcendentals=0),
        compiler_params=pltpu.CompilerParams(vmem_limit_bytes=16 * 1024 * 1024),
    )(queries, positives[None, :])


def kernel(first, last, block0, slots, scale, n_docs, n_asked, per, n_tiles, *refs):
    firsts = refs[0]
    doc_parts = refs[1 : 1 + n_docs]
    asked = refs[1 + n_docs : 1 + n_docs + n_asked]
    rest = refs[1 + n_docs + n_asked :]
    if not first:
        given, rest = rest[:4], rest[4:]
    if last:
        results, rest = rest[: n_asked // per], rest[n_asked // per :]
    top, total, hit, count, docs, tiles, scores, doc_here, tile_here = rest
    part_rows, feat = doc_parts[0].shape
    rows = docs.shape[1]
    factor = scale * LOG2E
    lanes = TILE_Q // LANES
    iota = lax.broadcasted_iota(jnp.int32, (8, LANES), 0)
    inside = rows // part_rows
    doc_copies = [
        pltpu.make_async_copy(p, docs.at[k // inside, pl.ds(k % inside * part_rows, part_rows)], doc_here.at[k])
        for k, p in enumerate(doc_parts)
    ]

    def fetch(i):
        deep = asked[i].shape[0] // PIECES
        for p in range(PIECES):
            at = pl.ds(p * deep, deep)
            pltpu.make_async_copy(asked[i].at[at], tiles.at[i, at], tile_here.at[i]).start()

    for copy in doc_copies[:inside]:
        copy.start()
    fetch(0)
    for copy in doc_copies[inside:]:
        copy.start()
    for i in range(1, AHEAD):
        fetch(i)

    def arrive(i):
        pltpu.make_async_copy(asked[0], tiles.at[i], tile_here.at[i]).wait()

    def multiply(t, i):
        scores[t % 2] = jnp.dot(docs[t % n_tiles], tiles[i, 0:feat, :], preferred_element_type=jnp.float32)

    def consume(t, i):
        j, where = t % n_tiles, t % 2
        at = [pl.ds(pl.multiple_of(i * TILE_Q + LANES * l, LANES), LANES) for l in range(lanes)]
        codes = tiles[i, feat : feat + EXTRA, :].astype(jnp.float32)
        codes = (codes[0:1, :] * LANES + codes[1:2, :]).astype(jnp.int32)
        want = [jnp.broadcast_to(codes[:, LANES * l : LANES * (l + 1)], (8, LANES)) for l in range(lanes)]
        old = [top[:, a] for a in at]
        new = list(old)
        found = [hit[:, a] for a in at]
        seen = count[...]
        for r in range(0, rows, 16):
            marks = docs[j, r : r + 16, 0:LANES].astype(jnp.float32)
            base = firsts[block0 + (j * rows + r) // slots]
            for h8 in (0, 8):
                mark = marks[h8 : h8 + 8]
                valid = mark == mark
                seen = seen + jnp.where(valid, 1.0, 0.0)
                index = iota + (base + (r + h8) % slots)
                for l in range(lanes):
                    part = (where, pl.ds(r + h8, 8), pl.ds(LANES * l, LANES))
                    s = jnp.where(valid, scores[part], LOW)
                    scores[part] = s
                    new[l] = jnp.maximum(new[l], s)
                    found[l] = jnp.where(index == want[l], s, found[l])
        acc = [total[:, a] * jnp.exp2((o - m) * factor) for a, o, m in zip(at, old, new)]
        for r in range(0, rows, 8):
            for l in range(lanes):
                s = scores[where, pl.ds(r, 8), pl.ds(LANES * l, LANES)]
                acc[l] = acc[l] + jnp.exp2((s - new[l]) * factor)
        for l in range(lanes):
            top[:, at[l]] = new[l]
            total[:, at[l]] = acc[l]
            hit[:, at[l]] = found[l]
        count[...] = seen

    if first:
        top[...] = jnp.full(top.shape, LOW, jnp.float32)
        for ref in (total, hit, count):
            ref[...] = jnp.zeros(ref.shape, jnp.float32)
    else:
        for ref, old in zip((top, total, hit, count), given):
            ref[...] = old[...]
    for copy in doc_copies[:inside]:
        copy.wait()
    arrive(0)
    multiply(0, 0)
    for copy in doc_copies[inside:]:
        copy.wait()

    def step(g, carry):
        n = UNROLL * n_tiles
        for t in range(n):
            i = g * UNROLL + t // n_tiles
            if t % n_tiles == 0:
                for k in range(AHEAD, n_asked):
                    pl.when(i + AHEAD == k)(functools.partial(fetch, k))
            if (t + 1) % n_tiles == 0:
                pl.when(i + 1 < n_asked)(functools.partial(arrive, jnp.minimum(i + 1, n_asked - 1)))
            multiply((t + 1) % n, jnp.minimum(g * UNROLL + (t + 1) // n_tiles, n_asked - 1))
            consume(t, i)
        return carry

    lax.fori_loop(0, n_asked // UNROLL, step, 0)
    if last:
        width = per * TILE_Q
        m = jnp.max(top[...], axis=0, keepdims=True)
        s = jnp.sum(total[...] * jnp.exp2((top[...] - m) * factor), axis=0, keepdims=True)
        p = jnp.sum(hit[...], axis=0, keepdims=True)
        seen = jnp.sum(count[...], axis=0, keepdims=True) * (1.0 / n_asked)
        seen = jnp.concatenate([seen] * (width // LANES), axis=1)
        for b, out in enumerate(results):
            at = slice(b * width, (b + 1) * width)
            out[0:1, :] = m[:, at]
            out[1:2, :] = s[:, at]
            out[2:3, :] = p[:, at]
            out[3:4, :] = seen


def chunk(docs, tile_rows, firsts, asked, per, carry, last, block0, slots, scale):
    deep = asked[0].shape[0]
    rows, feat = docs[0].shape
    width = len(asked) * TILE_Q
    n_tiles = len(docs) * rows // tile_rows
    state = [((8, width), jnp.float32)] * 3 + [((8, LANES), jnp.float32)]
    vmem, hbm = pl.BlockSpec(memory_space=pltpu.VMEM), pl.BlockSpec(memory_space=pltpu.HBM)
    scratch = [
        pltpu.VMEM((n_tiles, tile_rows, feat), jnp.bfloat16),
        pltpu.VMEM((len(asked), deep, TILE_Q), jnp.bfloat16),
        pltpu.VMEM((2, tile_rows, TILE_Q), jnp.float32),
        pltpu.SemaphoreType.DMA((len(docs),)),
        pltpu.SemaphoreType.DMA((len(asked),)),
    ]
    if last:
        out = [jax.ShapeDtypeStruct((4, per * TILE_Q), jnp.float32)] * (len(asked) // per)
        scratch = [pltpu.VMEM(*s) for s in state] + scratch
    else:
        out = [jax.ShapeDtypeStruct(*s) for s in state]
    work = len(docs) * rows * width
    return pl.pallas_call(
        functools.partial(kernel, carry is None, last, block0, slots, scale, len(docs), len(asked), per, n_tiles),
        out_shape=out,
        in_specs=[pl.BlockSpec(memory_space=pltpu.SMEM)]
        + [hbm] * (len(docs) + len(asked))
        + [vmem] * len(carry or ()),
        out_specs=[vmem] * len(out),
        scratch_shapes=scratch,
        cost_estimate=pl.CostEstimate(flops=2 * work * feat, bytes_accessed=2 * deep * width, transcendentals=work),
        compiler_params=pltpu.CompilerParams(vmem_limit_bytes=VMEM_LIMIT),
    )(firsts, *docs, *asked, *(carry or ()))


def losses_of(queries, documents, counts, positives):
    slots, feat = documents.shape
    scale = feat ** (-0.5)
    slot = lax.broadcasted_iota(jnp.int32, documents.shape, 0)
    buffer = jnp.where(slot < counts[0], documents, jnp.bfloat16(jnp.nan))
    asked = list(prepared(queries, positives))
    per = len(asked)
    for o in NEIGHBOURS:
        asked += [by_offset(asked[h], o) for h in range(per)]
    held = [(0, 0, 0)]
    for offsets in NEAR:
        pieces = [by_offset(buffer, o) for o in offsets]
        held = held + [a for o in offsets for a in moved(held, o)]
        buffer = jnp.concatenate([buffer] + pieces, axis=0)
    parts = [buffer] + [by_offset(buffer, o) for o in FAR]
    firsts = first_indices([held, sum([moved(held, o) for o in FAR], [])], slots)
    theirs = [to_partner(part) for part in parts]
    common = (firsts, asked, per)
    rows = buffer.shape[0]
    carry = chunk([parts[0], theirs[0]], rows, *common, None, False, 0, slots, scale)
    carry = chunk(parts[1:] + theirs[1:], 2 * rows, *common, carry, True, 2 * len(held), slots, scale)
    answers = [carry[0]] + [by_offset(a, [-v for v in o]) for a, o in zip(carry[1:], NEIGHBOURS)]
    top = functools.reduce(jnp.maximum, [a[0] for a in answers])
    total = sum(a[1] * jnp.exp((a[0] - top) * scale) for a in answers)
    hit = sum(a[2] for a in answers)
    seen = sum(a[3] for a in answers)
    return top * scale + jnp.log(total) - hit * scale - jnp.log(seen)


def solution(mesh):
    finer = Mesh(mesh.devices.reshape(2, 4, 2, 2, 8), AXES)
    return jax.shard_map(
        losses_of,
        mesh=finer,
        in_specs=(P(AXES, None), P(AXES, None), P(AXES), P(AXES)),
        out_specs=P(AXES),
        check_vma=False,
    )
```

time: 261 us -> 108 us (0.41)
  the two profiles are of different devices: /device:TPU:1 before, /device:TPU:16 now
where the time goes in v2:
time: 108 us; the launch traced here: 107 us
  waiting for transfers between devices  42.8 us (40%)
  starting transfers between devices  30.2 us (28%)
  Pallas kernels  26.8 us (25%)
  local copies, waits for them, and re-layouts  3.63 us (3%)
  other arithmetic  3.05 us (3%)
    ppermute x16, waiting for transfers between devices, by_offset(): return lax.ppermute(value, AXES, pairs)  42.7 us
    ppermute x16, starting transfers between devices, by_offset(): return lax.ppermute(value, AXES, pairs)  30.1 us
    pallas_call x2, Pallas kernels, chunk(): pl.pallas_call(functools.partial(kernel, carry is None, last, block0, slo...  26.3 us
    unnamed x33, local copies, waits for them, and re-layouts  3.62 us
  transfers between devices with their start and end apart: 20, of which 10 were waited for; matrix products, arithmetic and copies ran while one was open for 1% of the time, Pallas kernels for 9%

profile of v2, /device:TPU:16, one launch (start us, length us, event | category | flops | bytes accessed | tf_op | source)
XLA Modules:
  0.0 107.3 jit_solution(16000500459327508241)
XLA Ops:
  0.0 0.0 copy-start.8
  0.7 0.9 constant_dynamic-update-slice_fusion.4
  1.6 7.3 %collective-permute-start = (bf16[32,768]{1,0:T(8,128)(2,1)S(1)}, bf16[32,768]{1,0:T(8,128)(2,1)S(1)}, u32[]{:S(2)}, u32[]{:S(2)}) collective-permute-start(bf16[32,768]{1,0:T(8,128)(2,1)S(1)} %get-tuple-element.26), channel_id=1, source_target_pairs={{0,4},{16,20},{1,5},{17,21},{2,6},{18,22},{3,7},{19,23},{4,0},{20,... | collective-permute-start | bytes 147464 | tf_op jit(solution)/shard_map/ppermute | solution.py:46
  8.9 1.4 %copy-done = bf16[1024,768]{1,0:T(8,128)(2,1)S(1)} copy-done((bf16[1024,768]{1,0:T(8,128)(2,1)S(1)}, bf16[1024,768]{1,0:T(8,128)(2,1)}, u32[]{:S(2)}) %copy-start) | copy-done | bytes 1572888
  10.3 0.7 copy-done.1
  11.0 0.5 shard_map.82
  11.5 1.6 %collective-permute-start.10 = (bf16[784,512]{1,0:T(8,128)(2,1)S(1)}, bf16[784,512]{1,0:T(8,128)(2,1)S(1)}, u32[]{:S(2)}, u32[]{:S(2)}) collective-permute-start(bf16[784,512]{1,0:T(8,128)(2,1)S(1)} %get-tuple-element.15.refs_3_.refs_7_), channel_id=1, source_target_pairs={{0,128},{16,152},{1,129},{17,153},{2,130},{18,154},{3,131},{19,155... | collective-permute-start | bytes 2408456 | tf_op jit(solution)/shard_map/ppermute | solution.py:46
  13.0 0.0 collective-permute-done
  13.0 3.5 %collective-permute-start.1 = (bf16[64,768]{1,0:T(8,128)(2,1)S(1)}, bf16[64,768]{1,0:T(8,128)(2,1)S(1)}, u32[]{:S(2)}, u32[]{:S(2)}) collective-permute-start(bf16[64,768]{1,0:T(8,128)(2,1)S(1)} %pad_maximum_fusion), channel_id=1, source_target_pairs={{0,74},{16,94},{1,75},{17,95},{2,76},{18,88},{3,77},{19,89},{4,78}... | collective-permute-start | bytes 294920 | tf_op jit(solution)/shard_map/ppermute | solution.py:46
  16.5 4.7 %collective-permute-start.2 = (bf16[64,768]{1,0:T(8,128)(2,1)S(1)}, bf16[64,768]{1,0:T(8,128)(2,1)S(1)}, u32[]{:S(2)}, u32[]{:S(2)}) collective-permute-start(bf16[64,768]{1,0:T(8,128)(2,1)S(1)} %pad_maximum_fusion), channel_id=1, source_target_pairs={{0,175},{16,241},{1,168},{17,242},{2,169},{18,243},{3,170},{19,244... | collective-permute-start | bytes 294920 | tf_op jit(solution)/shard_map/ppermute | solution.py:46
  21.2 0.0 collective-permute-start.3
  21.2 5.5 %collective-permute-done.1 = bf16[64,768]{1,0:T(8,128)(2,1)S(1)} collective-permute-done((bf16[64,768]{1,0:T(8,128)(2,1)S(1)}, bf16[64,768]{1,0:T(8,128)(2,1)S(1)}, u32[]{:S(2)}, u32[]{:S(2)}) %collective-permute-start.1) | collective-permute-done | bytes 98336 | tf_op jit(solution)/shard_map/ppermute | solution.py:46
  26.7 0.0 collective-permute-done.2
  26.8 3.3 %collective-permute-done.3 = bf16[64,768]{1,0:T(8,128)(2,1)S(1)} collective-permute-done((bf16[64,768]{1,0:T(8,128)(2,1)S(1)}, bf16[64,768]{1,0:T(8,128)(2,1)S(1)}, u32[]{:S(2)}, u32[]{:S(2)}) %collective-permute-start.3) | collective-permute-done | bytes 98336 | tf_op jit(solution)/shard_map/ppermute | solution.py:46
  30.1 0.1 collective-permute-start.16
  30.2 2.3 %collective-permute-start.4 = (bf16[256,768]{1,0:T(8,128)(2,1)S(1)}, bf16[256,768]{1,0:T(8,128)(2,1)S(1)}, u32[]{:S(2)}, u32[]{:S(2)}) collective-permute-start(bf16[256,768]{1,0:T(8,128)(2,1)S(1)} %constant_dynamic-update-slice_fusion.refs_1_), channel_id=1, source_target_pairs={{0,160},{16,248},{1,161},{17,249},{2,162},{18,250},{3,163},{19,251... | collective-permute-start | bytes 1179656 | tf_op jit(solution)/shard_map/ppermute | solution.py:46
  32.5 1.9 %collective-permute-start.5 = (bf16[256,768]{1,0:T(8,128)(2,1)S(1)}, bf16[256,768]{1,0:T(8,128)(2,1)S(1)}, u32[]{:S(2)}, u32[]{:S(2)}) collective-permute-start(bf16[256,768]{1,0:T(8,128)(2,1)S(1)} %constant_dynamic-update-slice_fusion.refs_1_), channel_id=1, source_target_pairs={{0,232},{16,176},{1,233},{17,177},{2,234},{18,178},{3,235},{19,179... | collective-permute-start | bytes 1179656 | tf_op jit(solution)/shard_map/ppermute | solution.py:46
  34.4 0.0 collective-permute-start.6
  34.4 0.0 collective-permute-done.16.refs_2_
  34.4 0.1 collective-permute-start.11
  34.5 9.3 %collective-permute-done.4.refs_1_ = bf16[256,768]{1,0:T(8,128)(2,1)S(1)} collective-permute-done((bf16[256,768]{1,0:T(8,128)(2,1)S(1)}, bf16[256,768]{1,0:T(8,128)(2,1)S(1)}, u32[]{:S(2)}, u32[]{:S(2)}) %collective-permute-start.4) | collective-permute-done | bytes 393248 | tf_op jit(solution)/shard_map/ppermute | solution.py:46
  43.8 3.4 %collective-permute-start.12 = (bf16[784,512]{1,0:T(8,128)(2,1)S(1)}, bf16[784,512]{1,0:T(8,128)(2,1)}, u32[]{:S(2)}, u32[]{:S(2)}) collective-permute-start(bf16[784,512]{1,0:T(8,128)(2,1)S(1)} %get-tuple-element.15.refs_3_.refs_7_), channel_id=1, source_target_pairs={{0,32},{16,112},{1,33},{17,113},{2,34},{18,114},{3,35},{19,115},{4... | collective-permute-start | bytes 2408456 | tf_op jit(solution)/shard_map/ppermute | solution.py:46
  47.2 0.0 collective-permute-done.5.refs_2_
  47.2 0.6 collective-permute-start.13
  47.8 0.0 collective-permute-done.6.refs_3_
  47.9 0.0 collective-permute-start.14
  47.9 0.0 collective-permute-done.10.refs_5_.refs_9_
  47.9 0.1 copy-done.11
  48.0 0.0 collective-permute-start.15
  48.0 0.6 copy-done.12
  48.6 5.9 %collective-permute-done.11.refs_6_.refs_10_ = bf16[784,512]{1,0:T(8,128)(2,1)} collective-permute-done((bf16[784,512]{1,0:T(8,128)(2,1)S(1)}, bf16[784,512]{1,0:T(8,128)(2,1)}, u32[]{:S(2)}, u32[]{:S(2)}) %collective-permute-start.11) | collective-permute-done | bytes 802848 | tf_op jit(solution)/shard_map/ppermute | solution.py:46
  54.5 0.0 collective-permute-start.7
  54.5 2.4 %collective-permute-done.12.refs_7_.refs_11_ = bf16[784,512]{1,0:T(8,128)(2,1)} collective-permute-done((bf16[784,512]{1,0:T(8,128)(2,1)S(1)}, bf16[784,512]{1,0:T(8,128)(2,1)}, u32[]{:S(2)}, u32[]{:S(2)}) %collective-permute-start.12) | collective-permute-done | bytes 802848 | tf_op jit(solution)/shard_map/ppermute | solution.py:46
  56.9 8.6 %collective-permute-done.13.refs_8_.refs_12_ = bf16[784,512]{1,0:T(8,128)(2,1)} collective-permute-done((bf16[784,512]{1,0:T(8,128)(2,1)S(1)}, bf16[784,512]{1,0:T(8,128)(2,1)}, u32[]{:S(2)}, u32[]{:S(2)}) %collective-permute-start.13) | collective-permute-done | bytes 802848 | tf_op jit(solution)/shard_map/ppermute | solution.py:46
  65.5 0.0 collective-permute-start.9
  65.5 0.6 fusion.9.refs_0_
  66.2 3.8 %collective-permute-done.15.refs_10_.refs_14_ = bf16[784,512]{1,0:T(8,128)(2,1)} collective-permute-done((bf16[784,512]{1,0:T(8,128)(2,1)S(1)}, bf16[784,512]{1,0:T(8,128)(2,1)}, u32[]{:S(2)}, u32[]{:S(2)}) %collective-permute-start.15) | collective-permute-done | bytes 802848 | tf_op jit(solution)/shard_map/ppermute | solution.py:46
  70.0 8.8 %shard_map.83 = (f32[8,4096]{1,0:T(8,128)}, f32[8,4096]{1,0:T(8,128)}, f32[8,4096]{1,0:T(8,128)}, f32[8,128]{1,0:T(8,128)}) custom-call(s32[64]{0:T(128)} %fusion.9.refs_0_, bf16[256,768]{1,0:T(8,128)(2,1)} %copy-done.4, bf16[256,768]{1,0:T(8,128)(2,1)} %copy-done.13, bf16[784,512]{1,0:T(8,128)(2,1)} %copy-done.2, bf16[784,512]{1,0:T(8,128)(2,1)} %copy-done.3, ...), custom_call_target="tpu_custom_call" | custom-call | flops 3221225472 | bytes 6422528 | tf_op jit(solution)/shard_map/pallas_call | solution.py:236
  78.7 0.0 collective-permute-done.7.refs_4_
  78.8 0.8 copy-done.14
  79.5 17.6 %shard_map.84 = (f32[4,1024]{1,0:T(4,128)}, f32[4,1024]{1,0:T(4,128)}, f32[4,1024]{1,0:T(4,128)}, f32[4,1024]{1,0:T(4,128)}) custom-call(s32[64]{0:T(128)} %fusion.9.refs_0_, bf16[256,768]{1,0:T(8,128)(2,1)} %copy-done.10, bf16[256,768]{1,0:T(8,128)(2,1)} %copy-done.11, bf16[256,768]{1,0:T(8,128)(2,1)} %copy-done.12, bf16[256,768]{1,0:T(8,128)(2,1)} %copy-done.14, ...), custom_call_target="tpu_custom_call" | custom-call | flops 9663676416 | bytes 6422528 | tf_op jit(solution)/shard_map/pallas_call | solution.py:236
  97.1 3.3 %collective-permute-start.17 = (f32[4,1024]{1,0:T(4,128)}, f32[4,1024]{1,0:T(4,128)S(1)}, u32[]{:S(2)}, u32[]{:S(2)}) collective-permute-start(f32[4,1024]{1,0:T(4,128)} %get-tuple-element.22), channel_id=1, source_target_pairs={{0,136},{16,144},{1,137},{17,145},{2,138},{18,146},{3,139},{19,147... | collective-permute-start | bytes 49160 | tf_op jit(solution)/shard_map/ppermute | solution.py:46
  100.4 1.3 %collective-permute-start.18 = (f32[4,1024]{1,0:T(4,128)}, f32[4,1024]{1,0:T(4,128)S(1)}, u32[]{:S(2)}, u32[]{:S(2)}) collective-permute-start(f32[4,1024]{1,0:T(4,128)} %get-tuple-element.23), channel_id=1, source_target_pairs={{0,96},{16,48},{1,97},{17,49},{2,98},{18,50},{3,99},{19,51},{4,100... | collective-permute-start | bytes 49160 | tf_op jit(solution)/shard_map/ppermute | solution.py:46
  101.8 0.3 collective-permute-done.17
  102.1 2.3 %collective-permute-done.18 = f32[4,1024]{1,0:T(4,128)S(1)} collective-permute-done((f32[4,1024]{1,0:T(4,128)}, f32[4,1024]{1,0:T(4,128)S(1)}, u32[]{:S(2)}, u32[]{:S(2)}) %collective-permute-start.18) | collective-permute-done | bytes 16416 | tf_op jit(solution)/shard_map/ppermute | solution.py:46
  104.4 1.3 %collective-permute-done.19 = f32[4,1024]{1,0:T(4,128)S(1)} collective-permute-done((f32[4,1024]{1,0:T(4,128)}, f32[4,1024]{1,0:T(4,128)S(1)}, u32[]{:S(2)}, u32[]{:S(2)}) %collective-permute-start.19) | collective-permute-done | bytes 16416 | tf_op jit(solution)/shard_map/ppermute | solution.py:46
  105.7 0.9 fusion.1
  106.7 0.6 subtract_subtract_fusion
  (35 shorter events, 0.1 us)
Async XLA Ops:
  0.0 65.5 %copy-start.5 = (s32[64]{0:T(128)S(1)}, s32[64]{0:T(128)}, u32[]{:S(2)}) copy-start(s32[64]{0:T(128)} %constant.100.clone) | copy-start | bytes 772
  0.0 65.5 %copy-start.6 = (s32[64]{0:T(128)S(1)}, s32[64]{0:T(128)}, u32[]{:S(2)}) copy-start(s32[64]{0:T(128)} %constant.97.clone) | copy-start | bytes 772
  0.0 65.5 %copy-start.7 = (s32[64]{0:T(128)S(1)}, s32[64]{0:T(128)}, u32[]{:S(2)}) copy-start(s32[64]{0:T(128)} %constant.98.clone) | copy-start | bytes 772
  0.0 65.5 %copy-start.8 = (s32[64]{0:T(128)S(1)}, s32[64]{0:T(128)}, u32[]{:S(2)}) copy-start(s32[64]{0:T(128)} %constant.99.clone) | copy-start | bytes 772
  1.6 11.4 %collective-permute-start = (bf16[32,768]{1,0:T(8,128)(2,1)S(1)}, bf16[32,768]{1,0:T(8,128)(2,1)S(1)}, u32[]{:S(2)}, u32[]{:S(2)}) collective-permute-start(bf16[32,768]{1,0:T(8,128)(2,1)S(1)} %get-tuple-element.26), channel_id=1, source_target_pairs={{0,4},{16,20},{1,5},{17,21},{2,6},{18,22},{3,7},{19,23},{4,0},{20,... | collective-permute-start | bytes 147464 | tf_op jit(solution)/shard_map/ppermute | solution.py:46
  8.9 1.4 %copy-start = (bf16[1024,768]{1,0:T(8,128)(2,1)S(1)}, bf16[1024,768]{1,0:T(8,128)(2,1)}, u32[]{:S(2)}) copy-start(bf16[1024,768]{1,0:T(8,128)(2,1)} %queries_ref.1) | copy-start | bytes 4718596
  10.3 0.7 copy-start.1
  11.4 58.5 %copy-start.2 = (bf16[784,512]{1,0:T(8,128)(2,1)}, bf16[784,512]{1,0:T(8,128)(2,1)S(1)}, u32[]{:S(2)}) copy-start(bf16[784,512]{1,0:T(8,128)(2,1)S(1)} %get-tuple-element.15.refs_3_.refs_7_) | copy-start | bytes 2408452
  11.4 58.5 %copy-start.3 = (bf16[784,512]{1,0:T(8,128)(2,1)}, bf16[784,512]{1,0:T(8,128)(2,1)S(1)}, u32[]{:S(2)}) copy-start(bf16[784,512]{1,0:T(8,128)(2,1)S(1)} %get-tuple-element.16.refs_4_.refs_8_) | copy-start | bytes 2408452
  11.5 36.4 %collective-permute-start.10 = (bf16[784,512]{1,0:T(8,128)(2,1)S(1)}, bf16[784,512]{1,0:T(8,128)(2,1)S(1)}, u32[]{:S(2)}, u32[]{:S(2)}) collective-permute-start(bf16[784,512]{1,0:T(8,128)(2,1)S(1)} %get-tuple-element.15.refs_3_.refs_7_), channel_id=1, source_target_pairs={{0,128},{16,152},{1,129},{17,153},{2,130},{18,154},{3,131},{19,155... | collective-permute-start | bytes 2408456 | tf_op jit(solution)/shard_map/ppermute | solution.py:46
  13.0 13.7 %collective-permute-start.1 = (bf16[64,768]{1,0:T(8,128)(2,1)S(1)}, bf16[64,768]{1,0:T(8,128)(2,1)S(1)}, u32[]{:S(2)}, u32[]{:S(2)}) collective-permute-start(bf16[64,768]{1,0:T(8,128)(2,1)S(1)} %pad_maximum_fusion), channel_id=1, source_target_pairs={{0,74},{16,94},{1,75},{17,95},{2,76},{18,88},{3,77},{19,89},{4,78}... | collective-permute-start | bytes 294920 | tf_op jit(solution)/shard_map/ppermute | solution.py:46
  16.5 10.2 %collective-permute-start.2 = (bf16[64,768]{1,0:T(8,128)(2,1)S(1)}, bf16[64,768]{1,0:T(8,128)(2,1)S(1)}, u32[]{:S(2)}, u32[]{:S(2)}) collective-permute-start(bf16[64,768]{1,0:T(8,128)(2,1)S(1)} %pad_maximum_fusion), channel_id=1, source_target_pairs={{0,175},{16,241},{1,168},{17,242},{2,169},{18,243},{3,170},{19,244... | collective-permute-start | bytes 294920 | tf_op jit(solution)/shard_map/ppermute | solution.py:46
  21.2 8.8 %collective-permute-start.3 = (bf16[64,768]{1,0:T(8,128)(2,1)S(1)}, bf16[64,768]{1,0:T(8,128)(2,1)S(1)}, u32[]{:S(2)}, u32[]{:S(2)}) collective-permute-start(bf16[64,768]{1,0:T(8,128)(2,1)S(1)} %pad_maximum_fusion), channel_id=1, source_target_pairs={{0,225},{16,191},{1,226},{17,184},{2,227},{18,185},{3,228},{19,186... | collective-permute-start | bytes 294920 | tf_op jit(solution)/shard_map/ppermute | solution.py:46
  30.1 39.9 %copy-start.4 = (bf16[256,768]{1,0:T(8,128)(2,1)}, bf16[256,768]{1,0:T(8,128)(2,1)S(1)}, u32[]{:S(2)}) copy-start(bf16[256,768]{1,0:T(8,128)(2,1)S(1)} %constant_dynamic-update-slice_fusion.refs_1_) | copy-start | bytes 1179652
  30.1 4.3 %collective-permute-start.16 = (bf16[256,768]{1,0:T(8,128)(2,1)S(1)}, bf16[256,768]{1,0:T(8,128)(2,1)S(1)}, u32[]{:S(2)}, u32[]{:S(2)}) collective-permute-start(bf16[256,768]{1,0:T(8,128)(2,1)S(1)} %constant_dynamic-update-slice_fusion.refs_1_), channel_id=1, source_target_pairs={{0,16},{16,0},{1,17},{17,1},{2,18},{18,2},{3,19},{19,3},{4,20},{20... | collective-permute-start | bytes 1179656 | tf_op jit(solution)/shard_map/ppermute | solution.py:50
  30.2 13.6 %collective-permute-start.4 = (bf16[256,768]{1,0:T(8,128)(2,1)S(1)}, bf16[256,768]{1,0:T(8,128)(2,1)S(1)}, u32[]{:S(2)}, u32[]{:S(2)}) collective-permute-start(bf16[256,768]{1,0:T(8,128)(2,1)S(1)} %constant_dynamic-update-slice_fusion.refs_1_), channel_id=1, source_target_pairs={{0,160},{16,248},{1,161},{17,249},{2,162},{18,250},{3,163},{19,251... | collective-permute-start | bytes 1179656 | tf_op jit(solution)/shard_map/ppermute | solution.py:46
  32.5 14.7 %collective-permute-start.5 = (bf16[256,768]{1,0:T(8,128)(2,1)S(1)}, bf16[256,768]{1,0:T(8,128)(2,1)S(1)}, u32[]{:S(2)}, u32[]{:S(2)}) collective-permute-start(bf16[256,768]{1,0:T(8,128)(2,1)S(1)} %constant_dynamic-update-slice_fusion.refs_1_), channel_id=1, source_target_pairs={{0,232},{16,176},{1,233},{17,177},{2,234},{18,178},{3,235},{19,179... | collective-permute-start | bytes 1179656 | tf_op jit(solution)/shard_map/ppermute | solution.py:46
  34.4 13.4 %collective-permute-start.6 = (bf16[256,768]{1,0:T(8,128)(2,1)S(1)}, bf16[256,768]{1,0:T(8,128)(2,1)S(1)}, u32[]{:S(2)}, u32[]{:S(2)}) collective-permute-start(bf16[256,768]{1,0:T(8,128)(2,1)S(1)} %constant_dynamic-update-slice_fusion.refs_1_), channel_id=1, source_target_pairs={{0,2},{16,22},{1,3},{17,23},{2,4},{18,16},{3,5},{19,17},{4,6},{20,... | collective-permute-start | bytes 1179656 | tf_op jit(solution)/shard_map/ppermute | solution.py:46
  34.4 13.6 %copy-start.13 = (bf16[256,768]{1,0:T(8,128)(2,1)}, bf16[256,768]{1,0:T(8,128)(2,1)S(1)}, u32[]{:S(2)}) copy-start(bf16[256,768]{1,0:T(8,128)(2,1)S(1)} %collective-permute-done.16.refs_2_) | copy-start | bytes 1179652
  34.4 20.0 %collective-permute-start.11 = (bf16[784,512]{1,0:T(8,128)(2,1)S(1)}, bf16[784,512]{1,0:T(8,128)(2,1)}, u32[]{:S(2)}, u32[]{:S(2)}) collective-permute-start(bf16[784,512]{1,0:T(8,128)(2,1)S(1)} %get-tuple-element.16.refs_4_.refs_8_), channel_id=1, source_target_pairs={{0,128},{16,152},{1,129},{17,153},{2,130},{18,154},{3,131},{19,155... | collective-permute-start | bytes 2408456 | tf_op jit(solution)/shard_map/ppermute | solution.py:46
  43.8 34.9 %copy-start.10 = (bf16[256,768]{1,0:T(8,128)(2,1)}, bf16[256,768]{1,0:T(8,128)(2,1)S(1)}, u32[]{:S(2)}) copy-start(bf16[256,768]{1,0:T(8,128)(2,1)S(1)} %collective-permute-done.4.refs_1_) | copy-start | bytes 1179652
  43.8 13.1 %collective-permute-start.12 = (bf16[784,512]{1,0:T(8,128)(2,1)S(1)}, bf16[784,512]{1,0:T(8,128)(2,1)}, u32[]{:S(2)}, u32[]{:S(2)}) collective-permute-start(bf16[784,512]{1,0:T(8,128)(2,1)S(1)} %get-tuple-element.15.refs_3_.refs_7_), channel_id=1, source_target_pairs={{0,32},{16,112},{1,33},{17,113},{2,34},{18,114},{3,35},{19,115},{4... | collective-permute-start | bytes 2408456 | tf_op jit(solution)/shard_map/ppermute | solution.py:46
  47.2 0.7 copy-start.11
  47.2 18.3 %collective-permute-start.13 = (bf16[784,512]{1,0:T(8,128)(2,1)S(1)}, bf16[784,512]{1,0:T(8,128)(2,1)}, u32[]{:S(2)}, u32[]{:S(2)}) collective-permute-start(bf16[784,512]{1,0:T(8,128)(2,1)S(1)} %get-tuple-element.16.refs_4_.refs_8_), channel_id=1, source_target_pairs={{0,32},{16,112},{1,33},{17,113},{2,34},{18,114},{3,35},{19,115},{4... | collective-permute-start | bytes 2408456 | tf_op jit(solution)/shard_map/ppermute | solution.py:46
  47.9 0.7 copy-start.12
  47.9 18.3 %collective-permute-start.14 = (bf16[784,512]{1,0:T(8,128)(2,1)S(1)}, bf16[784,512]{1,0:T(8,128)(2,1)}, u32[]{:S(2)}, u32[]{:S(2)}) collective-permute-start(bf16[784,512]{1,0:T(8,128)(2,1)S(1)} %get-tuple-element.15.refs_3_.refs_7_), channel_id=1, source_target_pairs={{0,1},{16,23},{1,2},{17,16},{2,3},{18,17},{3,4},{19,18},{4,5},{20,... | collective-permute-start | bytes 2408456 | tf_op jit(solution)/shard_map/ppermute | solution.py:46
  48.0 22.0 %copy-start.9 = (bf16[784,512]{1,0:T(8,128)(2,1)}, bf16[784,512]{1,0:T(8,128)(2,1)S(1)}, u32[]{:S(2)}) copy-start(bf16[784,512]{1,0:T(8,128)(2,1)S(1)} %collective-permute-done.10.refs_5_.refs_9_) | copy-start | bytes 2408452
  48.0 22.0 %collective-permute-start.15 = (bf16[784,512]{1,0:T(8,128)(2,1)S(1)}, bf16[784,512]{1,0:T(8,128)(2,1)}, u32[]{:S(2)}, u32[]{:S(2)}) collective-permute-start(bf16[784,512]{1,0:T(8,128)(2,1)S(1)} %get-tuple-element.16.refs_4_.refs_8_), channel_id=1, source_target_pairs={{0,1},{16,23},{1,2},{17,16},{2,3},{18,17},{3,4},{19,18},{4,5},{20,... | collective-permute-start | bytes 2408456 | tf_op jit(solution)/shard_map/ppermute | solution.py:46
  54.5 24.3 %collective-permute-start.7 = (bf16[256,768]{1,0:T(8,128)(2,1)S(1)}, bf16[256,768]{1,0:T(8,128)(2,1)S(1)}, u32[]{:S(2)}, u32[]{:S(2)}) collective-permute-start(bf16[256,768]{1,0:T(8,128)(2,1)S(1)} %collective-permute-done.4.refs_1_), channel_id=1, source_target_pairs={{0,16},{16,0},{1,17},{17,1},{2,18},{18,2},{3,19},{19,3},{4,20},{20... | collective-permute-start | bytes 1179656 | tf_op jit(solution)/shard_map/ppermute | solution.py:50
  56.9 21.9 %collective-permute-start.8 = (bf16[256,768]{1,0:T(8,128)(2,1)}, bf16[256,768]{1,0:T(8,128)(2,1)}, u32[]{:S(2)}, u32[]{:S(2)}) collective-permute-start(bf16[256,768]{1,0:T(8,128)(2,1)} %copy-done.11), channel_id=1, source_target_pairs={{0,16},{16,0},{1,17},{17,1},{2,18},{18,2},{3,19},{19,3},{4,20},{20... | collective-permute-start | bytes 1179656 | tf_op jit(solution)/shard_map/ppermute | solution.py:50
  65.5 13.3 %collective-permute-start.9 = (bf16[256,768]{1,0:T(8,128)(2,1)}, bf16[256,768]{1,0:T(8,128)(2,1)}, u32[]{:S(2)}, u32[]{:S(2)}) collective-permute-start(bf16[256,768]{1,0:T(8,128)(2,1)} %copy-done.12), channel_id=1, source_target_pairs={{0,16},{16,0},{1,17},{17,1},{2,18},{18,2},{3,19},{19,3},{4,20},{20... | collective-permute-start | bytes 1179656 | tf_op jit(solution)/shard_map/ppermute | solution.py:50
  78.7 0.8 copy-start.14
  97.1 5.0 %collective-permute-start.17 = (f32[4,1024]{1,0:T(4,128)}, f32[4,1024]{1,0:T(4,128)S(1)}, u32[]{:S(2)}, u32[]{:S(2)}) collective-permute-start(f32[4,1024]{1,0:T(4,128)} %get-tuple-element.22), channel_id=1, source_target_pairs={{0,136},{16,144},{1,137},{17,145},{2,138},{18,146},{3,139},{19,147... | collective-permute-start | bytes 49160 | tf_op jit(solution)/shard_map/ppermute | solution.py:46
  100.4 3.9 %collective-permute-start.18 = (f32[4,1024]{1,0:T(4,128)}, f32[4,1024]{1,0:T(4,128)S(1)}, u32[]{:S(2)}, u32[]{:S(2)}) collective-permute-start(f32[4,1024]{1,0:T(4,128)} %get-tuple-element.23), channel_id=1, source_target_pairs={{0,96},{16,48},{1,97},{17,49},{2,98},{18,50},{3,99},{19,51},{4,100... | collective-permute-start | bytes 49160 | tf_op jit(solution)/shard_map/ppermute | solution.py:46
  101.8 3.9 %collective-permute-start.19 = (f32[4,1024]{1,0:T(4,128)}, f32[4,1024]{1,0:T(4,128)S(1)}, u32[]{:S(2)}, u32[]{:S(2)}) collective-permute-start(f32[4,1024]{1,0:T(4,128)} %get-tuple-element.24), channel_id=1, source_target_pairs={{0,7},{16,17},{1,0},{17,18},{2,1},{18,19},{3,2},{19,20},{4,3},{20,... | collective-permute-start | bytes 49160 | tf_op jit(solution)/shard_map/ppermute | solution.py:46
